TPU v7x, 512 devices: a whole 4x8x8 slice. The times are simulated.
512 devices in a mesh: dp: 64 (over y, z), aug: 8 (over x, core).
Axes of the slice: x: 4, y: 8, z: 8, core: 2. Of those that a mesh axis runs over, the one named last changes fastest.
Arguments:
- images: bfloat16 [8, 64, 197, 768], P('aug', 'dp'), may hold values from -6 to 6
- out_grads: bfloat16 [8, 64, 197, 768], P('aug', 'dp'), may hold values from -8 to 8
- up_weight_t: bfloat16 [3072, 768], P(('dp', 'aug')), may hold values from -0.21875 to 0.21875
- down_weight_t: bfloat16 [3072, 768], P(('dp', 'aug')), may hold values from -0.21875 to 0.21875
- left_up: bfloat16 [3072, 128], P(('dp', 'aug')), may hold values from -0.109375 to 0.109375
- right_up: bfloat16 [768, 128], replicated, may hold values from -0.21875 to 0.21875
- left_down: bfloat16 [768, 128], replicated, may hold values from -0.21875 to 0.21875
- right_down: bfloat16 [3072, 128], P(('dp', 'aug')), may hold values from -0.109375 to 0.109375
- noise: float32 [2, 128, 128], P(None, 'aug'), may hold values from -6 to 6
Outputs:
- update: float32 [2, 128, 128], P(None, 'aug')
- clip_scales: float32 [64], P('dp')
All inputs are finite; a program needn't handle non-finite values.
Results may differ from a plain program's by a relative error of at most 0.0032.
Values may be sent and summed in bfloat16 or wider, within the bound.
No kernel may reach another device: no remote copies, remote signals or barrier semaphores. Data moves between devices by JAX's collectives and lax.ppermute only.
A program may use at most 64 MiB of HBM per device.

v0:
```python
import math
import jax
import jax.numpy as jnp
from jax import lax
from jax.sharding import Mesh
from jax.sharding import PartitionSpec as P

DP = ("dp_0", "dp_1")
DP_AUG = ("dp_0", "dp_1", "aug")
gelu_coef = 0.7978845608028654
clip_frac = 0.3
noise_mult = 0.05


def side_by_side(arrays, axis, dim, along):
    ends, at = ([], 0)
    for a in arrays[:-1]:
        at += a.shape[along]
        ends.append(at)
    both = jnp.concatenate(arrays, axis=along)
    return tuple(jnp.split(lax.all_gather(both, axis, axis=dim, tiled=True), ends, axis=along))


def copy_for_each(shard, axis):
    size = lax.axis_size(axis)
    return lax.all_to_all(
        jnp.broadcast_to(shard[None], (size, *shard.shape)), axis, 0, 0, tiled=True
    )


def of_everyone(shard, axis):
    return copy_for_each(shard, axis).sum(axis=0)


def by_axis(shard, axes):
    for axis in axes:
        shard = lax.psum(shard, axis)
    return shard


def gelu_pair(hidden):
    inner = gelu_coef * (hidden + 0.044715 * hidden * hidden * hidden)
    tangent = jnp.tanh(inner)
    value = 0.5 * hidden * (1.0 + tangent)
    slope = 0.5 * (1.0 + tangent) + 0.5 * hidden * (1.0 - tangent * tangent) * gelu_coef * (
        1.0 + 3.0 * 0.044715 * hidden * hidden
    )
    return (value, slope)


def contract_last(left, right):
    return lax.dot_general(
        left, right, (((1,), (1,)), ((), ())), preferred_element_type=jnp.float32
    )


def local(
    images, out_grads, up_weight_t, down_weight_t, left_up, right_up, left_down, right_down, noise
):
    local_augs = images.shape[0]
    local_images = images.shape[1]
    tokens = images.shape[2]
    width = images.shape[3]
    rank = right_up.shape[1]
    token_rows = images.reshape(-1, width)
    grad_rows = out_grads.reshape(-1, width)
    grouped = side_by_side((up_weight_t, down_weight_t, left_up, right_down), "aug", 0, 1)
    up_piece, down_piece, left_piece, right_piece = side_by_side(
        (grouped[0], grouped[1], grouped[2], grouped[3]), DP, 0, 1
    )
    hidden = contract_last(token_rows, up_piece)
    activation, slope = gelu_pair(hidden)
    back = contract_last(grad_rows, down_piece)
    hidden_grad = (back * slope).astype(jnp.bfloat16)
    first = jnp.dot(hidden_grad, left_piece, preferred_element_type=jnp.float32)
    second = jnp.dot(
        activation.astype(jnp.bfloat16), right_piece, preferred_element_type=jnp.float32
    )
    up_total = first
    down_total = second
    v_up = up_total.astype(jnp.bfloat16)
    u_down = down_total.astype(jnp.bfloat16)
    u_up = jnp.dot(token_rows, right_up, preferred_element_type=jnp.float32).astype(jnp.bfloat16)
    v_down = jnp.dot(grad_rows, left_down, preferred_element_type=jnp.float32).astype(jnp.bfloat16)
    shape = (local_augs, local_images, tokens, rank)
    first = jnp.einsum(
        "aitr,aits->irs",
        v_up.reshape(shape),
        u_up.reshape(shape),
        preferred_element_type=jnp.float32,
    )
    second = jnp.einsum(
        "aitr,aits->irs",
        v_down.reshape(shape),
        u_down.reshape(shape),
        preferred_element_type=jnp.float32,
    )
    local_terms = jnp.stack([first, second], axis=1)
    all_augs = local_augs * lax.axis_size("aug")
    share_rows = rank // lax.axis_size("aug")
    lower_row = lax.axis_index("aug") * share_rows
    summed_terms = of_everyone(local_terms, "aug")
    aug_mean = summed_terms / all_augs
    squares = jnp.sum(aug_mean * aug_mean, axis=(1, 2, 3))
    my_rows = lax.dynamic_slice_in_dim(aug_mean, lower_row, share_rows, 2)
    norms = jnp.sqrt(squares + 1e-06)
    clip_norm = clip_frac * rank * math.sqrt(tokens / all_augs)
    clip_scales = jnp.minimum(1.0, clip_norm / norms)
    clipped_rows = jnp.sum(clip_scales[:, None, None, None] * my_rows, axis=0)
    summed_rows = by_axis(clipped_rows, DP)
    all_images = local_images * lax.axis_size(DP)
    update = (summed_rows + noise_mult * clip_norm * noise) / jnp.sqrt(jnp.float32(all_images))
    return (update, clip_scales)


def solution(mesh):
    torus = Mesh(mesh.devices.reshape(8, 8, mesh.shape["aug"]), ("dp_0", "dp_1", "aug"))
    placed = (
        P("aug", DP, None, None),
        P("aug", DP, None, None),
        P(DP_AUG, None),
        P(DP_AUG, None),
        P(DP_AUG, None),
        P(),
        P(),
        P(DP_AUG, None),
        P(None, "aug", None),
    )
    return jax.shard_map(
        local, mesh=torus, in_specs=placed, out_specs=(P(None, "aug", None), P(DP)), check_vma=False
    )
```

profile of v0, /device:TPU:2, one launch (start us, length us, event | category | flops | bytes accessed | tf_op | source)
XLA Modules:
  0.0 238.5 jit_solution(18309758157067267480)
XLA Ops:
  7.2 0.0 copy-start
  7.2 0.0 all-gather.3.cloned.1.call-start
  7.2 0.8 maximum_bitcast_fusion.1
  8.0 15.5 %all-gather = bf16[8,6,1792]{2,1,0:T(8,128)(2,1)S(1)} all-gather(bf16[1,6,1792]{2,1,0:T(8,128)(2,1)S(1)} %maximum_bitcast_fusion.1), channel_id=1, replica_groups=mesh['dp_0'=8,'dp_1'=8,'aug'=8] {'aug'}, dimensions={0}, use_global_device_ids=true | all-gather | bytes 193536 | tf_op jit(solution)/shard_map/all_gather | solution.py:21
  23.5 0.7 reshape.63
  24.3 0.0 all-gather.3.cloned.1.call-update
  24.3 0.0 copy-start.1
  24.3 113.4 %all-gather.3.cloned.1.call-done = bf16[3072,1792]{1,0:T(8,128)(2,1)} async-done(((bf16[48,1792]{1,0:T(8,128)(2,1)}), bf16[3072,1792]{1,0:T(8,128)(2,1)}) %all-gather.3.cloned.1.call-update) | async-done | bytes 11010064 | tf_op jit(solution)/shard_map/all_gather | solution.py:21
  137.7 0.0 copy-done
  137.7 4.0 %fusion.7 = f32[197,3072]{1,0:T(8,128)S(1)} fusion(bf16[3072,1792]{1,0:T(8,128)(2,1)} %all-gather.3.cloned.1.call-done, bf16[1,1,197,768]{3,2,1,0:T(8,128)(2,1)S(1)} %copy-done), kind=kOutput, calls=%fused_computation.5 | convolution fusion | flops 929562624 | bytes 7441920 | tf_op jit(solution)/shard_map/dot_general | solution.py:52
  141.7 0.0 copy-done.1
  141.7 0.0 copy-start.2
  141.7 5.3 %fusion.30 = bf16[197,128]{1,0:T(8,128)(2,1)S(1)} fusion(bf16[3072,1792]{1,0:T(8,128)(2,1)} %all-gather.3.cloned.1.call-done, f32[197,3072]{1,0:T(8,128)S(1)} %fusion.7, bf16[1,1,197,768]{3,2,1,0:T(8,128)(2,1)S(1)} %copy-done.1), kind=kOutput, calls=%fused_computation.23 | convolution fusion | flops 1096013440 | bytes 8278784 | tf_op jit(solution)/shard_map/dot_general | solution.py:75
  147.0 0.0 copy-done.2
  147.0 0.4 convolution_bitcast_fusion.1
  147.4 0.0 copy-start.3
  147.4 2.2 fusion.33
  149.6 0.0 copy-done.3
  149.6 0.5 convolution_bitcast_fusion
  150.1 0.0 copy-start.4
  150.1 1.1 broadcast_in_dim.10
  151.2 4.8 %all-to-all-start = ((f32[8,1,2,128,128]{4,3,2,1,0:T(8,128)}), f32[8,1,2,128,128]{4,3,2,1,0:T(8,128)S(1)}, u32[]{:S(2)}, u32[]{:S(2)}) async-start(f32[8,1,2,128,128]{4,3,2,1,0:T(8,128)} %broadcast_in_dim.10), calls=%async_computation | async-start | bytes 2097152 | tf_op jit(solution)/shard_map/all_to_all | solution.py:26
  156.0 14.5 %all-to-all-done = f32[8,1,2,128,128]{4,3,2,1,0:T(8,128)S(1)} async-done(((f32[8,1,2,128,128]{4,3,2,1,0:T(8,128)}), f32[8,1,2,128,128]{4,3,2,1,0:T(8,128)S(1)}, u32[]{:S(2)}, u32[]{:S(2)}) %all-to-all-start) | async-done | bytes 1048608 | tf_op jit(solution)/shard_map/all_to_all | solution.py:26
  170.5 0.1 reduce_sum.16
  170.5 0.6 multiply_reduce_fusion
  171.9 29.7 %psum.14 = f32[2,16,128]{2,1,0:T(8,128)S(1)} all-reduce(f32[2,16,128]{2,1,0:T(8,128)S(1)} %dynamic-slice_multiply_fusion), channel_id=1, replica_groups=mesh['dp_0'=8,'dp_1'=8,'aug'=8] {'dp_0'}, use_global_device_ids=true, to_apply=%region_2.0 | all-reduce | flops 4096 | bytes 32768 | tf_op jit(solution)/shard_map/psum | solution.py:37
  201.6 28.3 %psum.15 = f32[2,16,128]{2,1,0:T(8,128)S(1)} all-reduce(f32[2,16,128]{2,1,0:T(8,128)S(1)} %psum.14), channel_id=1, replica_groups=mesh['dp_0'=8,'dp_1'=8,'aug'=8] {'dp_1'}, use_global_device_ids=true, to_apply=%region_3.0 | all-reduce | flops 4096 | bytes 32768 | tf_op jit(solution)/shard_map/psum | solution.py:37
  229.9 0.0 copy-done.4
  229.9 0.6 add_multiply_fusion
  (2 shorter events, 0.0 us)
Async XLA Ops:
  7.2 130.6 %copy-start = (bf16[1,1,197,768]{3,2,1,0:T(8,128)(2,1)S(1)}, bf16[1,1,197,768]{3,2,1,0:T(8,128)(2,1)}, u32[]{:S(2)}) copy-start(bf16[1,1,197,768]{3,2,1,0:T(8,128)(2,1)} %param.9) | copy-start | bytes 907780
  7.2 130.6 %all-gather.3.cloned.1.call-start = ((), (), s32[]{:S(2)}) async-start(), calls=%async_computation.1 | async-start | bytes 11182080 | tf_op jit(solution)/shard_map/all_gather | solution.py:21
  24.3 117.4 %copy-start.1 = (bf16[1,1,197,768]{3,2,1,0:T(8,128)(2,1)S(1)}, bf16[1,1,197,768]{3,2,1,0:T(8,128)(2,1)}, u32[]{:S(2)}) copy-start(bf16[1,1,197,768]{3,2,1,0:T(8,128)(2,1)} %param.10) | copy-start | bytes 907780
  141.7 5.3 %copy-start.2 = (bf16[768,128]{1,0:T(8,128)(2,1)S(1)}, bf16[768,128]{1,0:T(8,128)(2,1)}, u32[]{:S(2)}) copy-start(bf16[768,128]{1,0:T(8,128)(2,1)} %param.14) | copy-start | bytes 589828
  147.4 2.2 copy-start.3
  150.1 79.8 %copy-start.4 = (f32[2,16,128]{2,1,0:T(8,128)S(1)}, f32[2,16,128]{2,1,0:T(8,128)}, u32[]{:S(2)}) copy-start(f32[2,16,128]{2,1,0:T(8,128)} %param.17) | copy-start | bytes 49156
  151.2 19.3 %all-to-all-start = ((f32[8,1,2,128,128]{4,3,2,1,0:T(8,128)}), f32[8,1,2,128,128]{4,3,2,1,0:T(8,128)S(1)}, u32[]{:S(2)}, u32[]{:S(2)}) async-start(f32[8,1,2,128,128]{4,3,2,1,0:T(8,128)} %broadcast_in_dim.10), calls=%async_computation | async-start | bytes 2097152 | tf_op jit(solution)/shard_map/all_to_all | solution.py:26
Sparse Core Ops, SparseCore 0:
  24.4 113.2 all-gather.2
where the time goes:
time: 239 us
  waiting for transfers between devices  128 us (54%)
  blocking collectives  73.6 us (31%)
  between operations  16 us (7%)
  matrix products  12.2 us (5%)
  starting transfers between devices  4.83 us (2%)
    all_gather x1, waiting for transfers between devices, side_by_side(): lax.all_gather(both, axis, axis=dim, tiled=True)  113 us
    psum x2, blocking collectives, by_axis(): shard = lax.psum(shard, axis)  58.1 us
    all_gather x1, blocking collectives, side_by_side(): lax.all_gather(both, axis, axis=dim, tiled=True)  15.5 us
    all_to_all x1, waiting for transfers between devices, copy_for_each(): lax.all_to_all(jnp.broadcast_to(shard[None], (size, *shard.shape)), axis,...  14.5 us
    dot_general x1, matrix products, local(): first = jnp.dot(hidden_grad, left_piece, preferred_element_type=jnp.float32)  5.26 us
    all_to_all x1, starting transfers between devices, copy_for_each(): lax.all_to_all(jnp.broadcast_to(shard[None], (size, *shard.shape)), axis,...  4.79 us
  transfers between devices with their start and end apart: 2, of which 2 were waited for; matrix products, arithmetic and copies ran while one was open for 0% of the time, Pallas kernels for 0%

commit v1 on v0

--- a/solution.py
+++ b/solution.py
@@ -10,6 +10,12 @@
 gelu_coef = 0.7978845608028654
 clip_frac = 0.3
 noise_mult = 0.05
+
+
+def add_all(array, axis):
+    shards = lax.all_gather(array, axis, axis=0, tiled=False)
+    result = shards.sum(axis=0)
+    return result
 
 
 def side_by_side(arrays, axis, dim, along):
@@ -34,7 +40,7 @@
 
 def by_axis(shard, axes):
     for axis in axes:
-        shard = lax.psum(shard, axis)
+        shard = add_all(shard, axis)
     return shard
 
 

time: 239 us -> 232 us (0.971)
  the two profiles are of different devices: /device:TPU:2 before, /device:TPU:16 now
where the time goes in v1:
time: 232 us; the launch traced here: 231 us
  waiting for transfers between devices  132 us (57%)
  blocking collectives  63.3 us (27%)
  between operations  16 us (7%)
  matrix products  12.2 us (5%)
  starting transfers between devices  4.29 us (2%)
    all_gather x1, waiting for transfers between devices, side_by_side(): lax.all_gather(both, axis, axis=dim, tiled=True)  116 us
    all_gather x2, blocking collectives, add_all(): shards = lax.all_gather(array, axis, axis=0, tiled=False)  50.1 us
    all_to_all x1, waiting for transfers between devices, copy_for_each(): lax.all_to_all(jnp.broadcast_to(shard[None], (size, *shard.shape)), axis,...  15.9 us
    all_gather x1, blocking collectives, side_by_side(): lax.all_gather(both, axis, axis=dim, tiled=True)  13.2 us
    dot_general x1, matrix products, local(): first = jnp.dot(hidden_grad, left_piece, preferred_element_type=jnp.float32)  5.26 us
  transfers between devices with their start and end apart: 2, of which 2 were waited for; matrix products, arithmetic and copies ran while one was open for 0% of the time, Pallas kernels for 0%

profile of v1, /device:TPU:16, one launch (start us, length us, event | category | flops | bytes accessed | tf_op | source)
XLA Modules:
  0.0 231.4 jit_solution(16102641114889778105)
XLA Ops:
  7.2 0.0 copy-start
  7.2 0.0 all-gather.5.cloned.1.call-start
  7.2 0.8 maximum_bitcast_fusion.1
  8.0 13.2 %all-gather.2 = bf16[8,6,1792]{2,1,0:T(8,128)(2,1)S(1)} all-gather(bf16[1,6,1792]{2,1,0:T(8,128)(2,1)S(1)} %maximum_bitcast_fusion.1), channel_id=1, replica_groups=mesh['dp_0'=8,'dp_1'=8,'aug'=8] {'aug'}, dimensions={0}, use_global_device_ids=true | all-gather | bytes 193536 | tf_op jit(solution)/shard_map/all_gather | solution.py:27
  21.2 0.7 reshape.65
  21.9 0.0 all-gather.5.cloned.1.call-update
  21.9 0.0 copy-start.1
  22.0 115.6 %all-gather.5.cloned.1.call-done = bf16[3072,1792]{1,0:T(8,128)(2,1)} async-done(((bf16[48,1792]{1,0:T(8,128)(2,1)}), bf16[3072,1792]{1,0:T(8,128)(2,1)}) %all-gather.5.cloned.1.call-update) | async-done | bytes 11010064 | tf_op jit(solution)/shard_map/all_gather | solution.py:27
  137.6 0.0 copy-done
  137.6 4.0 %fusion.7 = f32[197,3072]{1,0:T(8,128)S(1)} fusion(bf16[3072,1792]{1,0:T(8,128)(2,1)} %all-gather.5.cloned.1.call-done, bf16[1,1,197,768]{3,2,1,0:T(8,128)(2,1)S(1)} %copy-done), kind=kOutput, calls=%fused_computation.5 | convolution fusion | flops 929562624 | bytes 7441920 | tf_op jit(solution)/shard_map/dot_general | solution.py:58
  141.6 0.0 copy-done.1
  141.6 0.0 copy-start.2
  141.6 5.3 %fusion.30 = bf16[197,128]{1,0:T(8,128)(2,1)S(1)} fusion(bf16[3072,1792]{1,0:T(8,128)(2,1)} %all-gather.5.cloned.1.call-done, f32[197,3072]{1,0:T(8,128)S(1)} %fusion.7, bf16[1,1,197,768]{3,2,1,0:T(8,128)(2,1)S(1)} %copy-done.1), kind=kOutput, calls=%fused_computation.23 | convolution fusion | flops 1096013440 | bytes 8278784 | tf_op jit(solution)/shard_map/dot_general | solution.py:81
  146.8 0.0 copy-done.2
  146.9 0.4 convolution_bitcast_fusion.1
  147.3 0.0 copy-start.3
  147.3 2.2 fusion.33
  149.4 0.0 copy-done.3
  149.4 0.5 convolution_bitcast_fusion
  149.9 0.0 copy-start.4
  149.9 1.1 broadcast_in_dim.10
  151.0 4.3 %all-to-all-start = ((f32[8,1,2,128,128]{4,3,2,1,0:T(8,128)}), f32[8,1,2,128,128]{4,3,2,1,0:T(8,128)S(1)}, u32[]{:S(2)}, u32[]{:S(2)}) async-start(f32[8,1,2,128,128]{4,3,2,1,0:T(8,128)} %broadcast_in_dim.10), calls=%async_computation | async-start | bytes 2097152 | tf_op jit(solution)/shard_map/all_to_all | solution.py:32
  155.3 15.9 %all-to-all-done = f32[8,1,2,128,128]{4,3,2,1,0:T(8,128)S(1)} async-done(((f32[8,1,2,128,128]{4,3,2,1,0:T(8,128)}), f32[8,1,2,128,128]{4,3,2,1,0:T(8,128)S(1)}, u32[]{:S(2)}, u32[]{:S(2)}) %all-to-all-start) | async-done | bytes 1048608 | tf_op jit(solution)/shard_map/all_to_all | solution.py:32
  171.2 0.1 reduce_sum.40
  171.3 0.6 multiply_reduce_fusion
  172.6 25.5 %all-gather = f32[16,16,128]{2,1,0:T(8,128)S(1)} all-gather(f32[2,16,128]{2,1,0:T(8,128)S(1)} %dynamic-slice_multiply_fusion), channel_id=2, replica_groups=mesh['dp_0'=8,'dp_1'=8,'aug'=8] {'dp_0'}, dimensions={0}, use_global_device_ids=true | all-gather | bytes 147456 | tf_op jit(solution)/shard_map/all_gather | solution.py:16
  198.2 24.6 %all-gather.1 = f32[16,16,128]{2,1,0:T(8,128)S(1)} all-gather(f32[2,16,128]{2,1,0:T(8,128)S(1)} %reduce_sum.42), channel_id=3, replica_groups=mesh['dp_0'=8,'dp_1'=8,'aug'=8] {'dp_1'}, dimensions={0}, use_global_device_ids=true | all-gather | bytes 147456 | tf_op jit(solution)/shard_map/all_gather | solution.py:16
  222.8 0.0 copy-done.4
  222.8 0.6 add_multiply_fusion
  (4 shorter events, 0.1 us)
Async XLA Ops:
  7.2 130.4 %copy-start = (bf16[1,1,197,768]{3,2,1,0:T(8,128)(2,1)S(1)}, bf16[1,1,197,768]{3,2,1,0:T(8,128)(2,1)}, u32[]{:S(2)}) copy-start(bf16[1,1,197,768]{3,2,1,0:T(8,128)(2,1)} %param.9) | copy-start | bytes 907780
  7.2 130.4 %all-gather.5.cloned.1.call-start = ((), (), s32[]{:S(2)}) async-start(), calls=%async_computation.1 | async-start | bytes 11182080 | tf_op jit(solution)/shard_map/all_gather | solution.py:27
  21.9 119.6 %copy-start.1 = (bf16[1,1,197,768]{3,2,1,0:T(8,128)(2,1)S(1)}, bf16[1,1,197,768]{3,2,1,0:T(8,128)(2,1)}, u32[]{:S(2)}) copy-start(bf16[1,1,197,768]{3,2,1,0:T(8,128)(2,1)} %param.10) | copy-start | bytes 907780
  141.6 5.3 %copy-start.2 = (bf16[768,128]{1,0:T(8,128)(2,1)S(1)}, bf16[768,128]{1,0:T(8,128)(2,1)}, u32[]{:S(2)}) copy-start(bf16[768,128]{1,0:T(8,128)(2,1)} %param.14) | copy-start | bytes 589828
  147.3 2.2 copy-start.3
  149.9 72.8 %copy-start.4 = (f32[2,16,128]{2,1,0:T(8,128)S(1)}, f32[2,16,128]{2,1,0:T(8,128)}, u32[]{:S(2)}) copy-start(f32[2,16,128]{2,1,0:T(8,128)} %param.17) | copy-start | bytes 49156
  151.0 20.2 %all-to-all-start = ((f32[8,1,2,128,128]{4,3,2,1,0:T(8,128)}), f32[8,1,2,128,128]{4,3,2,1,0:T(8,128)S(1)}, u32[]{:S(2)}, u32[]{:S(2)}) async-start(f32[8,1,2,128,128]{4,3,2,1,0:T(8,128)} %broadcast_in_dim.10), calls=%async_computation | async-start | bytes 2097152 | tf_op jit(solution)/shard_map/all_to_all | solution.py:32
Sparse Core Ops, SparseCore 0:
  22.1 115.4 all-gather.4
